TPU v7x, 32 devices: a whole 2x2x4 slice. The times are simulated.
32 devices in a mesh: dp: 32 (over z, y, x, core).
Axes of the slice: x: 2, y: 2, z: 4, core: 2. Of those that a mesh axis runs over, the one named last changes fastest.
Arguments:
- gradients: bfloat16 [32, 48, 4608], P('dp'), may hold values from -144 to 144
- owned_rows: int32 [32], replicated, may hold values from 1 to 3, 48 in all
- master: float32 [96, 4608], P('dp'), may hold values from -0.09375 to 0.09375
- first_moment: float32 [96, 4608], P('dp'), may hold values from -0.03125 to 0.03125
- second_moment: float32 [96, 4608], P('dp'), may hold values from 1.3563368e-06 to 1.3563368e-05
Outputs:
- new_master: float32 [96, 4608], P('dp')
- new_first: float32 [96, 4608], P('dp')
- new_second: float32 [96, 4608], P('dp')
- direction: float32 [96, 4608], P('dp')
- weights: bfloat16 [48, 4608], replicated
Inputs may be any that keep to these rules, and one draw needn't show every extreme that they name: `owned_rows`: owners hold consecutive flat rows in owner order; the counts sum to 48 and some owner holds exactly 3.
All inputs are finite; a program needn't handle non-finite values.
Results may differ from a plain program's by a relative error of at most 0.001.
Values may be sent and summed in bfloat16 or wider, within the bound.
A program may use at most 128 MiB of HBM per device.

v0:
```python
import functools

import jax
import jax.numpy as jnp
from jax import lax
from jax.experimental import pallas as pl
from jax.experimental.pallas import tpu as pltpu
from jax.sharding import PartitionSpec as P

STEP = 100
beta_one = 0.9
beta_two = 0.999
adam_eps = 1e-08
learn_rate = 0.001
decay_rate = 0.1
clip_norm = 1.0

LANES = 128
SUBLANES = 8
MESH = pl.DeviceIdType.MESH


def adam(slot_grad, master, first, second, live):
    new_first = beta_one * first + (1.0 - beta_one) * slot_grad
    new_second = beta_two * second + (1.0 - beta_two) * slot_grad * slot_grad
    first_hat = new_first * (1.0 / (1.0 - beta_one**STEP))
    second_hat = new_second * (1.0 / (1.0 - beta_two**STEP))
    direction = first_hat / (jnp.sqrt(second_hat) + adam_eps) + decay_rate * master
    new_master = master - learn_rate * direction
    zero = jnp.zeros_like(new_master)
    return tuple(jnp.where(live, v, zero) for v in (new_master, new_first, new_second, direction))


def kernel(cfg, owned_ref, g_hbm, m_hbm, f_hbm, s_hbm,
           grad_hbm, w_hbm,
           g_buf, p0_land, pair, p1_land, p2_land, sel, st, st_land, ship, own_land,
           np_send, np_land, w_send, w_land, c_buf, stage, m_buf, f_buf, s_buf, grad_buf,
           g_sem, in_sem, out_sem, w_sem,
           p0_s, p0_r, p1_s, p1_r, st_s, st_r, p2_s, p2_r, sh_s, sh_r, np_s, np_r, p4_s, p4_r,
           p5_s, p5_r, fw_s, fw_r):
    n, group, lines, rows, cap, tiles, win, base = cfg
    me = lax.axis_index("dp")
    k = me % group
    z = me // group
    width = win * LANES
    slots = cap * group
    small = tiles // group
    head = (win + 1) // 2
    chunks = [(0, head), (head, win - head)] if win > head else [(0, win)]

    def col(j):
        return pl.multiple_of(((j * tiles) // group) * LANES, LANES)

    def at_col(j, first, count):
        return pl.ds(pl.multiple_of(col(j) + first * LANES, LANES), count * LANES)

    def xor(a, b):
        out = a
        bit = 1
        while bit <= b:
            if b & bit:
                out = out + bit - 2 * bit * ((a // bit) % 2)
            bit *= 2
        return out

    def plane(d):
        return z * group + xor(k, d)

    def line(d):
        return xor(z, d) * group + k

    load = pltpu.make_async_copy(g_hbm.at[0], g_buf, g_sem)
    load.start()
    states = [pltpu.make_async_copy(src, dst, in_sem.at[i]) for i, (src, dst) in
              enumerate(((m_hbm, m_buf), (f_hbm, f_buf), (s_hbm, s_buf)))]
    for copy in states:
        copy.start()
    barrier = pltpu.get_barrier_semaphore()
    for d in range(1, group):
        pl.semaphore_signal(barrier, inc=1, device_id=(plane(d),), device_id_type=MESH)
    for d in range(1, lines):
        pl.semaphore_signal(barrier, inc=1, device_id=(line(d),), device_id_type=MESH)
    pl.semaphore_wait(barrier, group - 1 + lines - 1)
    load.wait()

    def remote(src, dst, ssem, rsem, dev):
        return pltpu.make_async_remote_copy(
            src_ref=src, dst_ref=dst, send_sem=ssem, recv_sem=rsem,
            device_id=(dev,), device_id_type=MESH)

    started = []

    def launch(*args):
        copy = remote(*args)
        copy.start()
        started.append(copy)
        return copy

    order = sorted(range(1, group), key=lambda d: -bin(d).count("1"))
    far = list(range(lines - 1, 0, -1))
    chips = [d // 2 for d in order if d % 2 == 0]
    p0 = {}
    for e in chips + [0]:
        p0[e] = launch(g_buf.at[:, at_col(xor(k, 2 * e + 1), 0, win)], p0_land.at[e],
                       p0_s.at[e], p0_r.at[e], plane(1))
    p1 = {}
    for i, (first, count) in enumerate(chunks):
        lanes = pl.ds(first * LANES, count * LANES)
        for e in chips:
            if i == 0:
                p0[e].wait_recv()
            both = (g_buf[:, at_col(xor(k, 2 * e), first, count)].astype(jnp.float32)
                    + p0_land[e, :, lanes].astype(jnp.float32))
            pair[e, :, lanes] = both.astype(jnp.bfloat16)
            p1[i, e] = launch(pair.at[e, :, lanes], p1_land.at[e, :, lanes],
                              p1_s.at[i, e], p1_r.at[i, e], plane(2 * e))
    p0[0].wait_recv()

    for copy in states:
        copy.wait()
    st[...] = jnp.zeros_like(st)
    st[0:cap, :] = m_buf[...]
    st[cap:2 * cap, :] = f_buf[...]
    st[2 * cap:3 * cap, :] = s_buf[...]
    stc = {}
    for d in order:
        stc[d] = launch(st.at[:, at_col(xor(k, d), 0, win)], st_land.at[d],
                        st_s.at[d], st_r.at[d], plane(d))

    total = lines * slots
    q = lax.broadcasted_iota(jnp.int32, (total, n), 0)
    o = lax.broadcasted_iota(jnp.int32, (total, n), 1)
    q_owner = group * (q // slots) + q % group
    owned = jnp.broadcast_to(owned_ref[...], (total, n))
    count_q = jnp.sum(jnp.where(o == q_owner, owned, 0), axis=1, keepdims=True)
    start_q = jnp.sum(jnp.where(o < q_owner, owned, 0), axis=1, keepdims=True)
    q2 = lax.broadcasted_iota(jnp.int32, (total, rows), 0)
    r2 = lax.broadcasted_iota(jnp.int32, (total, rows), 1)
    j2 = (q2 % slots) // group
    hit = (r2 == start_q + j2) & (j2 < count_q)
    one_hot = jnp.where(hit, 1.0, 0.0)
    for i in range(lines):
        sel[i] = one_hot[i * slots:(i + 1) * slots]

    p2 = {}
    for i, (first, count) in enumerate(chunks):
        lanes = pl.ds(first * LANES, count * LANES)
        part = (g_buf[:, at_col(k, first, count)].astype(jnp.float32)
                + p0_land[0, :, lanes].astype(jnp.float32))
        for e in reversed(chips):
            p1[i, e].wait_recv()
            part = part + p1_land[e, :, lanes].astype(jnp.float32)
        p2_land[0, :, lanes] = part.astype(jnp.bfloat16)
        for d in far:
            p2[i, d] = launch(p2_land.at[0, :, lanes], p2_land.at[d, :, lanes],
                              p2_s.at[i, d], p2_r.at[i, d], line(d))

    for d in range(1, group):
        stc[d].wait_recv()
    for d in range(group):
        at = pl.ds(pl.multiple_of(xor(k, d) * base, SUBLANES), base)
        block = st[:, at_col(k, 0, win)] if d == 0 else st_land[d]
        for c in range(win):
            c_buf[c, at, :] = block[:, c * LANES:(c + 1) * LANES]

    own_width = ((k + 1) * tiles) // group - (k * tiles) // group
    norm_tile = jnp.zeros((SUBLANES, LANES), jnp.float32)
    for i, (first, count) in enumerate(chunks):
        lanes = pl.ds(first * LANES, count * LANES)
        whole = p2_land[0, :, lanes].astype(jnp.float32)
        for d in range(1, lines):
            p2[i, d].wait_recv()
            whole = whole + p2_land[d, :, lanes].astype(jnp.float32)
        squares = whole * whole
        for c in range(count):
            tile = squares[0:SUBLANES, c * LANES:(c + 1) * LANES]
            for r in range(1, rows // SUBLANES):
                tile = tile + squares[r * SUBLANES:(r + 1) * SUBLANES, c * LANES:(c + 1) * LANES]
            if first + c >= small:
                inside = jnp.full((SUBLANES, LANES), own_width, jnp.int32) > first + c
                tile = jnp.where(inside, tile, 0.0)
            norm_tile = norm_tile + tile
    np_send[...] = norm_tile
    np_land[k] = norm_tile
    npl = {}
    for d in order:
        npl[d] = launch(np_send, np_land.at[k], np_s.at[d], np_r.at[d], plane(d))

    my_sel = sel[z]
    live = jnp.sum(my_sel, axis=1, keepdims=True) > 0.5
    my_sel = my_sel.astype(jnp.bfloat16)
    summed = jnp.dot(my_sel, p2_land[0], preferred_element_type=jnp.float32)
    for d in range(1, lines):
        summed = summed + jnp.dot(my_sel, p2_land[d], preferred_element_type=jnp.float32)
    for j in range(cap):
        for c in range(win):
            ship[c, pl.ds(j, group, stride=SUBLANES), :] = summed[
                j * group:(j + 1) * group, c * LANES:(c + 1) * LANES]
    sh = {}
    for d in order:
        rows_to = pl.ds(pl.multiple_of(xor(k, d) * SUBLANES, SUBLANES), SUBLANES)
        sh[d] = launch(ship.at[:, rows_to, :], own_land.at[d],
                       sh_s.at[d], sh_r.at[d], plane(d))

    def state(a):
        return jnp.concatenate([
            jnp.concatenate([c_buf[c, pl.ds(a * cap + j, group, stride=base), :]
                             for c in range(win)], axis=1)
            for j in range(cap)], axis=0)

    master_c, first_c, second_c = state(0), state(1), state(2)
    for d in range(1, group):
        npl[d].wait_recv()
    tile = np_land[0]
    for i in range(1, group):
        tile = tile + np_land[i]
    norm_sq = jnp.sum(jnp.sum(tile, axis=0, keepdims=True), axis=1, keepdims=True)
    clip = jnp.minimum(1.0, clip_norm / (jnp.sqrt(norm_sq) + 1e-06))

    w_send[...] = adam(summed * clip, master_c, first_c, second_c, live)[0].astype(jnp.bfloat16)
    p4 = {}
    for i, (first, count) in enumerate(chunks):
        lanes = pl.ds(first * LANES, count * LANES)
        for d in far:
            p4[i, d] = launch(w_send.at[:, lanes], w_land.at[d, :, lanes],
                              p4_s.at[i, d], p4_r.at[i, d], line(d))

    for d in range(1, group):
        sh[d].wait_recv()
    for d in range(group):
        if d == 0:
            pieces = [ship[c, pl.ds(pl.multiple_of(k * SUBLANES, SUBLANES), SUBLANES), :]
                      for c in range(win)]
        else:
            pieces = [own_land[d, c] for c in range(win)]
        g_own = jnp.concatenate(pieces, axis=1)[0:cap]
        grad_buf[:, at_col(xor(k, d), 0, win)] = g_own * clip
    grad_out = pltpu.make_async_copy(grad_buf, grad_hbm, out_sem)
    grad_out.start()

    def spread(i, x):
        return lax.dot_general(sel[i].astype(jnp.bfloat16), x, (((0,), (0,)), ((), ())),
                               preferred_element_type=jnp.float32)

    def wide(j):
        return ((j + 1) * tiles) // group - (j * tiles) // group > small

    def final(src_k, first, count):
        return w_hbm.at[:, at_col(src_k, first, count)]

    local, inward = [], []

    def settle(i, e):
        src_k, from_k = xor(k, 2 * e), xor(k, 2 * e + 1)
        first, count = chunks[i]
        sure = min(count, small - first)
        parts = [(i, first, sure, None)] if sure > 0 else []
        if first + count > small:
            parts.append((2, small, 1, (wide(src_k), wide(from_k))))
        for t, begin, span, when in parts:
            src = stage.at[e, :, pl.ds(begin * LANES, span * LANES)]
            ahead = remote(src, final(src_k, begin, span), fw_s.at[t, e], fw_r.at[t, e], plane(1))
            here = pltpu.make_async_copy(src, final(src_k, begin, span), w_sem.at[t, e])
            if when is None:
                ahead.start()
                here.start()
            else:
                @pl.when(when[0])
                def _(ahead=ahead, here=here):
                    ahead.start()
                    here.start()
            back = remote(src, final(from_k, begin, span), fw_s.at[t, e], fw_r.at[t, e], plane(1))
            local.append((ahead, here, when))
            inward.append((back, when))

    p5 = {}
    for i, (first, count) in enumerate(chunks):
        lanes = pl.ds(first * LANES, count * LANES)
        flat = spread(z, w_send[:, lanes])
        for d in range(1, lines):
            p4[i, d].wait_recv()
            flat = flat + spread(xor(z, d), w_land[d, :, lanes])
        stage[0, :, lanes] = flat.astype(jnp.bfloat16)
        for e in chips:
            p5[i, e] = launch(stage.at[0, :, lanes], stage.at[e, :, lanes],
                              p5_s.at[i, e], p5_r.at[i, e], plane(2 * e))
        settle(i, 0)
    for i in range(len(chunks)):
        for e in reversed(chips):
            p5[i, e].wait_recv()
            settle(i, e)
    grad_out.wait()
    for back, when in inward:
        if when is None:
            back.wait_recv()
        else:
            pl.when(when[1])(back.wait_recv)
    for ahead, here, when in local:
        def done(ahead=ahead, here=here):
            ahead.wait_send()
            here.wait()
        if when is None:
            done()
        else:
            pl.when(when[0])(done)
    for copy in started:
        copy.wait_send()


def finish(owned_ref, g_ref, m_ref, f_ref, s_ref, w_ref,
           nm_ref, nf_ref, ns_ref, dr_ref, out_ref):
    out_ref[...] = w_ref[...]
    me = lax.axis_index("dp")
    cap = m_ref.shape[0]
    o = lax.broadcasted_iota(jnp.int32, owned_ref.shape, 1)
    count = jnp.sum(jnp.where(o == me, owned_ref[...], 0), axis=1, keepdims=True)
    live = lax.broadcasted_iota(jnp.int32, m_ref.shape, 0) < count
    outs = adam(g_ref[...], m_ref[...], f_ref[...], s_ref[...], live)
    for ref, v in zip((nm_ref, nf_ref, ns_ref, dr_ref), outs):
        ref[...] = v


def per_device(n, gradients, owned_rows, master, first_moment, second_moment):
    rows, width_all = gradients.shape[1:]
    cap = master.shape[0]
    group = 8
    while n % group:
        group //= 2
    lines = n // group
    tiles = width_all // LANES
    win = -(-tiles // group)
    width = win * LANES
    slots = cap * group
    base = -(-3 * cap // SUBLANES) * SUBLANES
    cfg = (n, group, lines, rows, cap, tiles, win, base)
    f32, b16 = jnp.float32, jnp.bfloat16
    sds = jax.ShapeDtypeStruct((cap, width_all), f32)
    weights_type = jax.ShapeDtypeStruct((rows, width_all), b16)
    vm = pl.BlockSpec(memory_space=pltpu.VMEM)
    anym = pl.BlockSpec(memory_space=pl.ANY)
    dma = pltpu.SemaphoreType.DMA
    scratch = [
        pltpu.VMEM((rows, width_all), b16),
        pltpu.VMEM((group // 2, rows, width), b16),
        pltpu.VMEM((group // 2, rows, width), b16),
        pltpu.VMEM((group // 2, rows, width), b16),
        pltpu.VMEM((lines, rows, width), b16),
        pltpu.VMEM((lines, slots, rows), f32),
        pltpu.VMEM((base, width_all), f32),
        pltpu.VMEM((group, base, width), f32),
        pltpu.VMEM((win, group * SUBLANES, LANES), f32),
        pltpu.VMEM((group, win, SUBLANES, LANES), f32),
        pltpu.VMEM((SUBLANES, LANES), f32),
        pltpu.VMEM((group, SUBLANES, LANES), f32),
        pltpu.VMEM((slots, width), b16),
        pltpu.VMEM((lines, slots, width), b16),
        pltpu.VMEM((win, group * base, LANES), f32),
        pltpu.VMEM((group // 2, rows, width), b16),
        pltpu.VMEM((cap, width_all), f32),
        pltpu.VMEM((cap, width_all), f32),
        pltpu.VMEM((cap, width_all), f32),
        pltpu.VMEM((cap, width_all), f32),
        dma, dma((3,)), dma, dma((3, group // 2)),
        dma((group // 2,)), dma((group // 2,)),
        dma((2, group // 2)), dma((2, group // 2)), dma((group,)), dma((group,)),
        dma((2, lines)), dma((2, lines)), dma((group,)), dma((group,)),
        dma((group,)), dma((group,)), dma((2, lines)), dma((2, lines)),
        dma((2, group // 2)), dma((2, group // 2)), dma((3, group // 2)), dma((3, group // 2)),
    ]
    owned = owned_rows.reshape(1, n)
    slot_grad, gathered = pl.pallas_call(
        functools.partial(kernel, cfg),
        out_shape=(sds, weights_type),
        in_specs=[vm, anym, anym, anym, anym],
        out_specs=(anym, anym),
        scratch_shapes=scratch,
        compiler_params=pltpu.CompilerParams(collective_id=0, has_side_effects=True),
    )(owned, gradients, master, first_moment, second_moment)
    return pl.pallas_call(
        finish,
        out_shape=(sds, sds, sds, sds, weights_type),
        in_specs=[vm] * 6,
        out_specs=(vm,) * 5,
    )(owned, slot_grad, master, first_moment, second_moment, gathered)


def solution(mesh):
    in_specs = (P("dp", None, None), P(), P("dp", None), P("dp", None), P("dp", None))
    out_specs = (P("dp", None), P("dp", None), P("dp", None), P("dp", None), P())
    return jax.shard_map(
        functools.partial(per_device, mesh.shape["dp"]),
        mesh=mesh, in_specs=in_specs, out_specs=out_specs, check_vma=False
    )
```

profile of v0, /device:TPU:0, one launch (start us, length us, event | category | flops | bytes accessed | tf_op | source)
XLA Modules:
  0.0 35.2 jit_solution(15447015791305953147)
XLA Ops:
  0.6 32.4 %shard_map.92 = (f32[3,4608]{1,0:T(4,128)}, bf16[48,4608]{1,0:T(8,128)(2,1)}) custom-call(s32[1,32]{1,0:T(1,128)} %bitcast.1, bf16[1,48,4608]{2,1,0:T(8,128)(2,1)} %g_hbm.1, f32[3,4608]{1,0:T(4,128)} %m_ref.1, f32[3,4608]{1,0:T(4,128)} %f_ref.1, f32[3,4608]{1,0:T(4,128)} %s_ref.1), custom_call_target="tpu_custom_call" | custom-call | tf_op jit(solution)/shard_map/pallas_call | solution.py:371
  33.0 2.1 %shard_map.93 = (f32[3,4608]{1,0:T(4,128)}, f32[3,4608]{1,0:T(4,128)}, f32[3,4608]{1,0:T(4,128)}, f32[3,4608]{1,0:T(4,128)}, bf16[48,4608]{1,0:T(8,128)(2,1)}) custom-call(s32[1,32]{1,0:T(1,128)} %bitcast.2, f32[3,4608]{1,0:T(4,128)} %get-tuple-element.7.g_ref, f32[3,4608]{1,0:T(4,128)} %m_ref.1, f32[3,4608]{1,0:T(4,128)} %f_ref.1, f32[3,4608]{1,0:T(4,128)} %s_ref.1, ...), custom_call_target="tpu_custom_call" | custom-call | tf_op jit(solution)/shard_map/pallas_call | solution.py:379
where the time goes:
time: 35.3 us; the launch traced here: 35.2 us
  Pallas kernels  34.5 us (98%)
  between operations  0.64 us (2%)
    pallas_call x1, Pallas kernels, per_device(): pl.pallas_call(functools.partial(kernel, cfg), out_shape=(sds, weights_ty...  32.4 us
    pallas_call x1, Pallas kernels, per_device(): pl.pallas_call(finish, out_shape=(sds, sds, sds, sds, weights_type), in_s...  2.15 us

commit v1 on v0

--- a/solution.py
+++ b/solution.py
@@ -323,7 +323,7 @@
 def per_device(n, gradients, owned_rows, master, first_moment, second_moment):
     rows, width_all = gradients.shape[1:]
     cap = master.shape[0]
-    group = 8
+    group = 16
     while n % group:
         group //= 2
     lines = n // group

time: 35.3 us -> 35.9 us (1.017)
  Pallas kernels: 34.5 us -> 35.1 us
    pallas_call x1, Pallas kernels: 32.4 us -> 33 us  [per_device(): pl.pallas_call(functools.partial(kernel, cfg), out_shape=(sds, weights_ty...]
where the time goes in v1:
time: 35.9 us; the launch traced here: 35.7 us
  Pallas kernels  35.1 us (98%)
  between operations  0.64 us (2%)
    pallas_call x1, Pallas kernels, per_device(): pl.pallas_call(functools.partial(kernel, cfg), out_shape=(sds, weights_ty...  33 us
    pallas_call x1, Pallas kernels, per_device(): pl.pallas_call(finish, out_shape=(sds, sds, sds, sds, weights_type), in_s...  2.15 us

profile of v1, /device:TPU:0, one launch (start us, length us, event | category | flops | bytes accessed | tf_op | source)
XLA Modules:
  0.0 35.7 jit_solution(10397186390048023381)
XLA Ops:
  0.6 33.0 %shard_map.92 = (f32[3,4608]{1,0:T(4,128)}, bf16[48,4608]{1,0:T(8,128)(2,1)}) custom-call(s32[1,32]{1,0:T(1,128)} %bitcast.1, bf16[1,48,4608]{2,1,0:T(8,128)(2,1)} %g_hbm.1, f32[3,4608]{1,0:T(4,128)} %m_ref.1, f32[3,4608]{1,0:T(4,128)} %f_ref.1, f32[3,4608]{1,0:T(4,128)} %s_ref.1), custom_call_target="tpu_custom_call" | custom-call | tf_op jit(solution)/shard_map/pallas_call | solution.py:371
  33.6 2.1 %shard_map.93 = (f32[3,4608]{1,0:T(4,128)}, f32[3,4608]{1,0:T(4,128)}, f32[3,4608]{1,0:T(4,128)}, f32[3,4608]{1,0:T(4,128)}, bf16[48,4608]{1,0:T(8,128)(2,1)}) custom-call(s32[1,32]{1,0:T(1,128)} %bitcast.2, f32[3,4608]{1,0:T(4,128)} %get-tuple-element.7.g_ref, f32[3,4608]{1,0:T(4,128)} %m_ref.1, f32[3,4608]{1,0:T(4,128)} %f_ref.1, f32[3,4608]{1,0:T(4,128)} %s_ref.1, ...), custom_call_target="tpu_custom_call" | custom-call | tf_op jit(solution)/shard_map/pallas_call | solution.py:379

commit v2 on v1

v2 whole, which is shorter than its diff:
```python
import functools

import jax
import jax.numpy as jnp
from jax import lax
from jax.experimental import pallas as pl
from jax.experimental.pallas import tpu as pltpu
from jax.sharding import PartitionSpec as P

STEP = 100
beta_one = 0.9
beta_two = 0.999
adam_eps = 1e-08
learn_rate = 0.001
decay_rate = 0.1
clip_norm = 1.0

LANES = 128
SUBLANES = 8
PACK = 16
VMEM_BYTES = 67043328
MESH = pl.DeviceIdType.MESH


def adam(slot_grad, master, first, second):
    new_first = beta_one * first + (1.0 - beta_one) * slot_grad
    new_second = beta_two * second + (1.0 - beta_two) * slot_grad * slot_grad
    first_hat = new_first * (1.0 / (1.0 - beta_one**STEP))
    second_hat = new_second * (1.0 / (1.0 - beta_two**STEP))
    direction = first_hat / (jnp.sqrt(second_hat) + adam_eps) + decay_rate * master
    new_master = master - learn_rate * direction
    return new_master, new_first, new_second, direction


def xor(a, b, top):
    out = 0
    bit = 1
    while bit < top:
        out = out + bit * (((a // bit) + (b // bit)) % 2)
        bit *= 2
    return out


def extra_table(group, extra):
    even = [t for t in range(group // 2) if bin(t).count("1") % 2 == 0]
    half = extra // 2
    assert extra % 2 == 0 and extra <= len(even)
    return [[even[core * half + i] for i in range(half)] for core in range(2)]


def kernel(cfg, owned_hbm, g_hbm, m_hbm, f_hbm, s_hbm,
           nm_ref, nf_ref, ns_ref, dr_ref, w_ref,
           owned_v, grad_ref, g_buf, m_buf, f_buf, s_buf, st32, st, st_all, flat,
           p0_land, pair, p1_land, h, p0x_land, pairx, p1x_land, hx,
           np_send, np_land, ship, own_land, shipx, own_landx,
           own_sem, g_sem, in_sem,
           p0_s, p0_r, p0x_s, p0x_r, p1_s, p1_r, p1x_s, p1x_r,
           h_s, h_r, hx_s, hx_r, ln_s, ln_r, st_s, st_r, stx_s, stx_r,
           np_s, np_r, sh_s, sh_r, shx_s, shx_r,
           ag_s, ag_r, agx_s, agx_r, fw_s, fw_r, fwx_s, fwx_r):
    n, group, lines, rows, cap, tiles, main, extra = cfg
    half = extra // 2
    table = extra_table(group, extra)
    base = group * main
    f32, b16 = jnp.float32, jnp.bfloat16
    me = lax.axis_index("dp")
    k = me % group
    z = me // group
    chip = k // 2
    core = k % 2
    nchips = group // 2
    slots = cap * group
    mw = main * LANES

    def main_at(j):
        return pl.ds(pl.multiple_of(j * mw, LANES), mw)

    def tile_at(t, count=1):
        return pl.ds(pl.multiple_of(t * LANES, LANES), count * LANES)

    def plane(d):
        return z * group + xor(k, d, group)

    def line(d):
        return xor(z, d, lines) * group + k

    def holder(c, i):
        return table[0][i] + c * (table[1][i] - table[0][i])

    mine = [chip == holder(core, i) for i in range(half)]
    i_me = 0
    wide = False
    for i in range(half):
        i_me = i_me + i * jnp.where(mine[i], 1, 0)
        wide = jnp.logical_or(wide, mine[i])

    owned_cp = pltpu.make_async_copy(owned_hbm, owned_v, own_sem)
    load = pltpu.make_async_copy(g_hbm.at[0], g_buf, g_sem)
    load.start()
    states = [pltpu.make_async_copy(src, dst, in_sem.at[i]) for i, (src, dst) in
              enumerate(((m_hbm, m_buf), (f_hbm, f_buf), (s_hbm, s_buf)))]
    for copy in states:
        copy.start()
    owned_cp.start()
    barrier = pltpu.get_barrier_semaphore()
    for d in range(1, group):
        pl.semaphore_signal(barrier, inc=1, device_id=(plane(d),), device_id_type=MESH)
    for d in range(1, lines):
        pl.semaphore_signal(barrier, inc=1, device_id=(line(d),), device_id_type=MESH)
    pl.semaphore_wait(barrier, group - 1 + lines - 1)
    load.wait()

    def remote(src, dst, ssem, rsem, dev):
        return pltpu.make_async_remote_copy(
            src_ref=src, dst_ref=dst, send_sem=ssem, recv_sem=rsem,
            device_id=(dev,), device_id_type=MESH)

    started = []

    def launch(*args, when=None):
        copy = remote(*args)
        if when is None:
            copy.start()
        else:
            pl.when(when)(copy.start)
        started.append((copy, when))
        return copy

    def on(when, action):
        if when is None:
            action()
        else:
            pl.when(when)(action)

    far = sorted(range(1, nchips), key=lambda e: -bin(e).count("1"))
    peers = sorted(range(1, group), key=lambda d: -bin(d).count("1"))

    p0 = {}
    p0x = launch(g_buf.at[:, tile_at(base + (1 - core) * half, half)], p0x_land, p0x_s, p0x_r, plane(1))
    for e in far + [0]:
        j = 2 * xor(chip, e, nchips) + 1 - core
        p0[e] = launch(g_buf.at[:, main_at(j)], p0_land.at[e], p0_s.at[e], p0_r.at[e], plane(1))

    for copy in states:
        copy.wait()
    owned_cp.wait()

    def split(x):
        high = x.astype(b16).astype(f32)
        return high, x - high

    mh, ml = split(m_buf[...])
    fh, fl = split(f_buf[...])
    st32[...] = jnp.zeros_like(st32)
    for i, part in enumerate((mh, ml, fh, fl, s_buf[...])):
        st32[i * cap:(i + 1) * cap, :] = part
    st[0] = st32[...].astype(b16)

    p0x.wait_recv()
    pairx[...] = (g_buf[:, tile_at(base + core * half, half)].astype(f32) + p0x_land[...].astype(f32)).astype(b16)
    for i in range(half):
        t = holder(core, i)
        dist = xor(chip, t, nchips)
        launch(pairx.at[:, i * LANES:(i + 1) * LANES], p1x_land.at[dist], p1x_s.at[i], p1x_r.at[dist],
               z * group + 2 * t + core, when=jnp.logical_not(mine[i]))
    p1 = {}
    for e in far:
        p0[e].wait_recv()
        j = 2 * xor(chip, e, nchips) + core
        pair[e] = (g_buf[:, main_at(j)].astype(f32) + p0_land[e].astype(f32)).astype(b16)
        p1[e] = launch(pair.at[e], p1_land.at[e], p1_s.at[e], p1_r.at[e], plane(2 * e))

    ln = {}
    for d in range(1, lines):
        ln[d] = launch(st.at[0], st.at[d], ln_s.at[d], ln_r.at[d], line(d))

    stw = {}
    stx_when = [jnp.logical_not(jnp.logical_and(chip == table[e // half][e % half], core == e // half))
                for e in range(extra)]

    def spread_state(l):
        for d in peers:
            at = pl.ds((l * group + d) * PACK, PACK)
            stw[l, d] = launch(st.at[l, :, main_at(xor(k, d, group))], st_all.at[at, 0:mw],
                               st_s.at[l, d], st_r.at[l, d], plane(d))
        for e in range(extra):
            j = 2 * table[e // half][e % half] + e // half
            dist = xor(k, j, group)
            at = pl.ds(pl.multiple_of((l * group + dist) * PACK, PACK), PACK)
            launch(st.at[l, :, tile_at(base + e)], st_all.at[at, mw:mw + LANES],
                   stx_s.at[l, e], stx_r.at[l, dist], z * group + j, when=stx_when[e])

    spread_state(0)

    unit = group * PACK
    q = lax.broadcasted_iota(jnp.int32, (1, unit), 1)
    part_q = q % PACK
    slot_q = part_q % cap
    kind_q = part_q // cap
    number = lax.broadcasted_iota(jnp.int32, (n, unit), 0)
    square = (n, n)
    diagonal = lax.broadcasted_iota(jnp.int32, square, 0) == lax.broadcasted_iota(jnp.int32, square, 1)
    column = jnp.sum(jnp.where(diagonal, jnp.broadcast_to(owned_v[...], square), 0), axis=1, keepdims=True)
    owned = jnp.broadcast_to(column, (n, unit))
    row = lax.broadcasted_iota(jnp.int32, (rows, unit), 0)

    def row_of(owner, slot):
        shape = owned.shape
        owner = jnp.broadcast_to(owner, shape)
        count = jnp.sum(jnp.where(number == owner, owned, 0), axis=0, keepdims=True)
        start = jnp.sum(jnp.where(number < owner, owned, 0), axis=0, keepdims=True)
        return jnp.where(slot < count, start + slot, -1)

    def picks(l):
        owner = xor(l, z, lines) * group + ((q // PACK) ^ k)
        at = jnp.where(kind_q < 5, row_of(owner, slot_q), -1)
        hit = row == jnp.broadcast_to(at, row.shape)
        kind = jnp.broadcast_to(kind_q // 2, row.shape)
        return jnp.concatenate(
            [jnp.where(jnp.logical_and(hit, kind == i), 1.0, 0.0) for i in range(3)], axis=0).astype(b16)

    q2 = lax.broadcasted_iota(jnp.int32, (1, unit), 1)
    at2 = jnp.where(q2 < slots, row_of(z * group + ((q2 % group) ^ k), q2 // group), -1)
    sel = jnp.where(row == jnp.broadcast_to(at2, row.shape), 1.0, 0.0)[:, 0:slots].astype(b16)

    part = g_buf[:, main_at(k)].astype(f32)
    p0[0].wait_recv()
    part = part + p0_land[0].astype(f32)
    for e in reversed(far):
        p1[e].wait_recv()
        part = part + p1_land[e].astype(f32)
    h[0] = part.astype(b16)
    hc = {}
    for d in range(1, lines):
        hc[d] = launch(h.at[0], h.at[d], h_s.at[d], h_r.at[d], line(d))

    @pl.when(wide)
    def _():
        total = pairx[:, tile_at(i_me)].astype(f32)
        for e in reversed(far):
            remote(pairx.at[:, 0:LANES], p1x_land.at[e], p1x_s.at[0], p1x_r.at[e], plane(2 * e)).wait_recv()
            total = total + p1x_land[e].astype(f32)
        hx[0] = total.astype(b16)

    hxc = {}
    for d in range(1, lines):
        hxc[d] = launch(hx.at[0], hx.at[d], hx_s.at[d], hx_r.at[d], line(d), when=wide)

    for d in range(1, lines):
        ln[d].wait_recv()
        spread_state(d)

    def merged(ref):
        total = ref[xor(z, 0, lines)].astype(f32)
        for l in range(1, lines):
            total = total + ref[xor(z, l, lines)].astype(f32)
        return total

    def norm_part(x):
        squares = x * x
        tile = jnp.zeros((SUBLANES, LANES), f32)
        for c in range(x.shape[1] // LANES):
            for r in range(rows // SUBLANES):
                tile = tile + squares[r * SUBLANES:(r + 1) * SUBLANES, c * LANES:(c + 1) * LANES]
        return tile

    for d in range(1, lines):
        hc[d].wait_recv()
    summed = merged(h)
    np_send[...] = norm_part(summed)

    @pl.when(wide)
    def _():
        for d in range(1, lines):
            hxc[d].wait_recv()
        np_send[...] = np_send[...] + norm_part(merged(hx))

    np_land[k] = np_send[...]
    npl = {}
    for d in peers:
        npl[d] = launch(np_send, np_land.at[k], np_s.at[d], np_r.at[d], plane(d))

    def slots_of(ref):
        def one(l):
            return lax.dot_general(sel, ref[xor(z, l, lines)], (((0,), (0,)), ((), ())),
                                   preferred_element_type=f32)
        total = one(0)
        for l in range(1, lines):
            total = total + one(l)
        return total

    picked = slots_of(h)
    block = own_land.shape[1]
    for j in range(cap):
        for c in range(main):
            ship[pl.ds(c * cap + j, group, stride=block), :] = picked[
                j * group:(j + 1) * group, c * LANES:(c + 1) * LANES]
    sh = {}
    for d in peers:
        sh[d] = launch(ship.at[pl.ds(d * block, block), :], own_land.at[d], sh_s.at[d], sh_r.at[d], plane(d))

    @pl.when(wide)
    def _():
        pickedx = slots_of(hx)
        for j in range(cap):
            shipx[pl.ds(j, group, stride=SUBLANES), :] = pickedx[j * group:(j + 1) * group, :]
        own_landx[core * half + i_me] = shipx[0:SUBLANES, :]

    for d in peers:
        launch(shipx.at[pl.ds(d * SUBLANES, SUBLANES), :], own_landx.at[core * half + i_me],
               shx_s.at[d], shx_r.at[core * half + i_me], plane(d), when=wide)

    for l in range(lines):
        for d in range(1, group):
            stw[l, d].wait_recv()
        st_all[pl.ds(l * group * PACK, PACK), 0:mw] = st[l, :, main_at(k)]

        @pl.when(wide)
        def _(l=l):
            for d in range(1, group):
                at = pl.ds((l * group + d) * PACK, PACK)
                remote(st.at[l, :, 0:LANES], st_all.at[at, mw:mw + LANES],
                       stx_s.at[l, 0], stx_r.at[l, d], plane(d)).wait_recv()
            st_all[pl.ds(l * group * PACK, PACK), mw:mw + LANES] = st[l, :, tile_at(base + core * half + i_me)]

    def bring(l, total):
        at = pl.ds(pl.multiple_of(l * unit, unit), unit)
        return total + jnp.dot(picks(l), st_all[at, :], preferred_element_type=f32)

    zero = jnp.zeros((3 * rows, mw + LANES), f32)
    if lines <= 2:
        total = zero
        for l in range(lines):
            total = bring(l, total)
        flat[...] = total
    else:
        flat[...] = zero

        def step(l, carry):
            flat[...] = bring(l, flat[...])
            return carry
        lax.fori_loop(0, lines, step, 0)

    for d in range(1, group):
        npl[d].wait_recv()
    tile = np_land[0]
    for i in range(1, group):
        tile = tile + np_land[i]
    norm_sq = jnp.sum(jnp.sum(tile, axis=0, keepdims=True), axis=1, keepdims=True)
    clip = jnp.minimum(1.0, clip_norm / (jnp.sqrt(norm_sq) + 1e-06))

    def updated(x, lanes):
        return adam(x * clip, flat[0:rows, lanes], flat[rows:2 * rows, lanes],
                    flat[2 * rows:3 * rows, lanes])[0].astype(b16)

    w_ref[:, main_at(k)] = updated(merged(h), slice(0, mw))
    ag, fw = {}, {}
    for e in far:
        ag[e] = launch(w_ref.at[:, main_at(k)], w_ref.at[:, main_at(k)], ag_s.at[e], ag_r.at[e], plane(2 * e))
    fw[0] = launch(w_ref.at[:, main_at(k)], w_ref.at[:, main_at(k)], fw_s.at[0], fw_r.at[0], plane(1))

    own_tile = tile_at(base + core * half + i_me)

    @pl.when(wide)
    def _():
        w_ref[:, own_tile] = updated(merged(hx), slice(mw, mw + LANES))

    for e in far:
        launch(w_ref.at[:, own_tile], w_ref.at[:, own_tile], agx_s.at[e], agx_r.at[i_me], plane(2 * e), when=wide)

    for d in range(group):
        if d == 0:
            got = ship[0:block, :]
        else:
            sh[d].wait_recv()
            got = own_land[d]
        piece = jnp.concatenate([got[c * cap:(c + 1) * cap] for c in range(main)], axis=1)
        grad_ref[:, main_at(xor(k, d, group))] = piece * clip
    for e in range(extra):
        j = 2 * table[e // half][e % half] + e // half

        @pl.when(stx_when[e])
        def _(e=e):
            remote(shipx.at[0:SUBLANES, :], own_landx.at[e], shx_s.at[1], shx_r.at[e], plane(1)).wait_recv()
        grad_ref[:, (base + e) * LANES:(base + e + 1) * LANES] = own_landx[e, 0:cap, :] * clip

    own_row = lax.broadcasted_iota(jnp.int32, (1, n), 1)
    count = jnp.sum(jnp.where(own_row == me, owned_v[...], 0), axis=1, keepdims=True)
    live = lax.broadcasted_iota(jnp.int32, m_buf.shape, 0) < count
    outs = adam(grad_ref[...], m_buf[...], f_buf[...], s_buf[...])
    for ref, v in zip((nm_ref, nf_ref, ns_ref, dr_ref), outs):
        ref[...] = jnp.where(live, v, jnp.zeros_like(v))

    def forward_main(e):
        at = main_at(2 * xor(chip, e, nchips) + core)
        if e:
            remote(w_ref.at[:, at], w_ref.at[:, at], ag_s.at[e], ag_r.at[e], plane(2 * e)).wait_recv()
            fw[e] = launch(w_ref.at[:, at], w_ref.at[:, at], fw_s.at[e], fw_r.at[e], plane(1))

    for e in reversed(far):
        forward_main(e)
    for i in range(half):
        at = tile_at(base + core * half + i)

        @pl.when(jnp.logical_not(mine[i]))
        def _(i=i, at=at):
            remote(w_ref.at[:, at], w_ref.at[:, at], agx_s.at[1], agx_r.at[i], plane(2)).wait_recv()
        launch(w_ref.at[:, at], w_ref.at[:, at], fwx_s.at[i], fwx_r.at[i], plane(1))

    for e in [0] + far[::-1]:
        at = main_at(2 * xor(chip, e, nchips) + 1 - core)
        remote(w_ref.at[:, at], w_ref.at[:, at], fw_s.at[e], fw_r.at[e], plane(1)).wait_recv()
    for i in range(half):
        at = tile_at(base + (1 - core) * half + i)
        remote(w_ref.at[:, at], w_ref.at[:, at], fwx_s.at[i], fwx_r.at[i], plane(1)).wait_recv()
    for copy, when in started:
        on(when, copy.wait_send)


def finish(*refs):
    count = (len(refs) - 1) // 2
    sem = refs[-1]
    copies = [pltpu.make_async_copy(refs[i], refs[count + i], sem.at[i]) for i in range(count)]
    for copy in copies:
        copy.start()
    for copy in copies:
        copy.wait()


def per_device(n, gradients, owned_rows, master, first_moment, second_moment):
    rows, width_all = gradients.shape[1:]
    cap = master.shape[0]
    group = 16
    while n % group:
        group //= 2
    lines = n // group
    tiles = width_all // LANES
    main = tiles // group
    extra = tiles - main * group
    cfg = (n, group, lines, rows, cap, tiles, main, extra)
    half = extra // 2
    chips = group // 2
    mw = main * LANES
    block = -(-cap * main // SUBLANES) * SUBLANES
    f32, b16 = jnp.float32, jnp.bfloat16
    sds = jax.ShapeDtypeStruct((cap, width_all), f32)
    weights_type = jax.ShapeDtypeStruct((rows, width_all), b16)
    vm = pl.BlockSpec(memory_space=pltpu.VMEM)
    dma = pltpu.SemaphoreType.DMA
    scratch = [
        pltpu.VMEM((1, n), jnp.int32),
        pltpu.VMEM((cap, width_all), f32),
        pltpu.VMEM((rows, width_all), b16),
        pltpu.VMEM((cap, width_all), f32),
        pltpu.VMEM((cap, width_all), f32),
        pltpu.VMEM((cap, width_all), f32),
        pltpu.VMEM((PACK, width_all), f32),
        pltpu.VMEM((lines, PACK, width_all), b16),
        pltpu.VMEM((lines * group * PACK, mw + LANES), b16),
        pltpu.VMEM((3 * rows, mw + LANES), f32),
        pltpu.VMEM((chips, rows, mw), b16),
        pltpu.VMEM((chips, rows, mw), b16),
        pltpu.VMEM((chips, rows, mw), b16),
        pltpu.VMEM((lines, rows, mw), b16),
        pltpu.VMEM((rows, half * LANES), b16),
        pltpu.VMEM((rows, half * LANES), b16),
        pltpu.VMEM((chips, rows, LANES), b16),
        pltpu.VMEM((lines, rows, LANES), b16),
        pltpu.VMEM((SUBLANES, LANES), f32),
        pltpu.VMEM((group, SUBLANES, LANES), f32),
        pltpu.VMEM((group * block, LANES), f32),
        pltpu.VMEM((group, block, LANES), f32),
        pltpu.VMEM((group * SUBLANES, LANES), f32),
        pltpu.VMEM((extra, SUBLANES, LANES), f32),
        dma, dma, dma((3,)),
        dma((chips,)), dma((chips,)), dma, dma, dma((chips,)), dma((chips,)), dma((half,)), dma((chips,)),
        dma((lines,)), dma((lines,)), dma((lines,)), dma((lines,)), dma((lines,)), dma((lines,)),
        dma((lines, group)), dma((lines, group)), dma((lines, extra)), dma((lines, group)),
        dma((group,)), dma((group,)), dma((group,)), dma((group,)), dma((group,)), dma((extra,)),
        dma((chips,)), dma((chips,)), dma((chips,)), dma((half,)),
        dma((chips,)), dma((chips,)), dma((half,)), dma((half,)),
    ]
    owned = owned_rows.reshape(1, n)
    room = VMEM_BYTES - rows * width_all * 2 - 16 * width_all * 4 - (32 << 10)
    hbm = pl.BlockSpec(memory_space=pltpu.HBM)
    outs = (sds,) * 4 + (weights_type,)
    made = pl.pallas_call(
        functools.partial(kernel, cfg),
        out_shape=tuple(pltpu.VMEM(o.shape, o.dtype) for o in outs),
        in_specs=[hbm] * 5,
        out_specs=(vm,) * 5,
        scratch_shapes=scratch,
        compiler_params=pltpu.CompilerParams(collective_id=0, has_side_effects=True, vmem_limit_bytes=room),
    )(owned, gradients, master, first_moment, second_moment)
    return pl.pallas_call(
        finish,
        out_shape=outs,
        in_specs=[vm] * 5,
        out_specs=(hbm,) * 5,
        scratch_shapes=[dma((5,))],
        compiler_params=pltpu.CompilerParams(vmem_limit_bytes=4 << 20),
    )(*made)


def solution(mesh):
    in_specs = (P("dp", None, None), P(), P("dp", None), P("dp", None), P("dp", None))
    out_specs = (P("dp", None), P("dp", None), P("dp", None), P("dp", None), P())
    return jax.shard_map(
        functools.partial(per_device, mesh.shape["dp"]),
        mesh=mesh, in_specs=in_specs, out_specs=out_specs, check_vma=False
    )
```

time: 35.9 us -> 31.3 us (0.87)
  Pallas kernels: 35.1 us -> 30.4 us
    pallas_call x2, Pallas kernels: 35.1 us -> 30.4 us  [the longest x1 29.5 us: per_device(): pl.pallas_call(functools.partial(kernel, cfg), out_shape=tuple((pltpu.VME...]
where the time goes in v2:
time: 31.3 us; the launch traced here: 31.1 us
  Pallas kernels  30.4 us (97%)
  between operations  0.64 us (2%)
    pallas_call x1, Pallas kernels, per_device(): pl.pallas_call(functools.partial(kernel, cfg), out_shape=tuple((pltpu.VME...  29.5 us
    pallas_call x1, Pallas kernels, per_device(): pl.pallas_call(finish, out_shape=outs, in_specs=[vm] * 5, out_specs=(hbm,...  0.91 us

profile of v2, /device:TPU:0, one launch (start us, length us, event | category | flops | bytes accessed | tf_op | source)
XLA Modules:
  0.0 31.1 jit_solution(12765961996657300013)
XLA Ops:
  0.6 29.5 %shard_map.92 = (f32[3,4608]{1,0:T(4,128)S(1)}, f32[3,4608]{1,0:T(4,128)S(1)}, f32[3,4608]{1,0:T(4,128)S(1)}, f32[3,4608]{1,0:T(4,128)S(1)}, bf16[48,4608]{1,0:T(8,128)(2,1)S(1)}) custom-call(s32[1,32]{1,0:T(1,128)} %bitcast.1, bf16[1,48,4608]{2,1,0:T(8,128)(2,1)} %g_hbm.1, f32[3,4608]{1,0:T(4,128)} %m_hbm.1, f32[3,4608]{1,0:T(4,128)} %f_hbm.1, f32[3,4608]{1,0:T(4,128)} %s_hbm.1), custom_call_target="tpu_custom_call" | custom-call | tf_op jit(solution)/shard_map/pallas_call | solution.py:487
  30.2 0.9 %shard_map.93 = (f32[3,4608]{1,0:T(4,128)}, f32[3,4608]{1,0:T(4,128)}, f32[3,4608]{1,0:T(4,128)}, f32[3,4608]{1,0:T(4,128)}, bf16[48,4608]{1,0:T(8,128)(2,1)}) custom-call(f32[3,4608]{1,0:T(4,128)S(1)} %get-tuple-element.10.refs_0_, f32[3,4608]{1,0:T(4,128)S(1)} %get-tuple-element.11.refs_1_, f32[3,4608]{1,0:T(4,128)S(1)} %get-tuple-element.12.refs_2_, ...), custom_call_target="tpu_custom_call" | custom-call | tf_op jit(solution)/shard_map/pallas_call | solution.py:495
